TPU v7x, 32 devices: a whole 2x2x4 slice. The times are simulated.
32 devices in a mesh: grid: 16 (over z, x, core), band: 2 (over y).
Axes of the slice: x: 2, y: 2, z: 4, core: 2. Of those that a mesh axis runs over, the one named last changes fastest.
Arguments:
- left_bands: float32 [2, 8, 128, 128, 128], P(None, 'band', 'grid'), may hold values from -6 to 6
- right_bands: float32 [2, 4, 128, 128, 128], P(None, 'band', 'grid'), may hold values from -6 to 6
- sphere_index: int32 [16384], replicated, may hold values from 0 to 2097151, as said below
- right_order: int32 [4], replicated, may hold values from 0 to 3, each once
Outputs:
- pair_density: float32 [2, 8, 4, 16384], P(None, 'band', None, 'grid')
Inputs may be any that keep to these rules, and one draw needn't show every extreme that they name: `sphere_index`: flat index (kz * 128 + ky) * 128 + kx; an index may repeat. In each aligned block of 1024 entries, at most 64 entries share one value of ky // 8, and some value is shared by exactly 64. `right_order`: each second band once.
All inputs are finite; a program needn't handle non-finite values.
Results may differ from a plain program's by a relative error of at most 0.00008.
Values sent between devices are 32-bit elements; how exact they have to be, the bound alone decides.
A program may use at most 256 MiB of HBM per device.

v0:
```python
import math

import jax
import jax.numpy as jnp
from jax import lax
from jax.experimental import pallas as pl
from jax.experimental.pallas import tpu as pltpu
from jax.sharding import PartitionSpec as P

HIGH = lax.Precision.HIGH
HIGHEST = lax.Precision.HIGHEST
F32 = jnp.float32
BF16 = jnp.bfloat16


def swapped(block, axis):
    count = lax.axis_size(axis)
    return lax.ppermute(block, axis, [(k, k ^ 1) for k in range(count)])


def dft_tables(length):
    counter = jnp.arange(length, dtype=jnp.int32)
    angles = (counter[:, None] * counter[None, :] % length).astype(F32) * (2.0 * math.pi / length)
    return (jnp.cos(angles), jnp.sin(angles))


def complex_matrix(length):
    cosine, sine = dft_tables(length)
    return jnp.concatenate(
        [jnp.concatenate([cosine, -sine], 1), jnp.concatenate([sine, cosine], 1)], 0
    ).reshape(2, length, 2, length)


def split(value):
    high = lax.reduce_precision(value, 8, 7)
    return high.astype(BF16), (value - high).astype(BF16)


def plan(sphere_index, grid, nx, n_dev):
    rows = grid // n_dev
    per = sphere_index.shape[0] // n_dev
    slots = max(1, per // n_dev)
    wave_z = sphere_index // (grid * nx)
    wave_y = sphere_index // nx % grid
    wave_x = sphere_index % nx
    source = (wave_y // rows).reshape(n_dev, per)
    onehot = (source[:, :, None] == jnp.arange(n_dev, dtype=jnp.int32)).astype(BF16)
    before = jnp.tril(jnp.ones((per, per), BF16), -1)
    counts = jnp.einsum("ij,bjs->bis", before, onehot, preferred_element_type=F32)
    rank = jnp.sum(counts * onehot, axis=2).astype(jnp.int32)
    slot = source * slots + rank
    column = (wave_y % rows) * nx + wave_x
    packed = (wave_z * (rows * nx) + column).reshape(n_dev, per)
    target = jnp.arange(n_dev * slots, dtype=jnp.int32)
    chosen = jnp.sum(
        jnp.where(slot[:, :, None] == target[None, None, :], packed[:, :, None] + 1, 0), axis=1
    ) - 1
    bits = n_dev.bit_length() - 1
    if n_dev == 1 << bits:
        chosen = chosen.reshape((2,) * bits + (n_dev * slots,))
        chosen = chosen.transpose(tuple(range(bits))[::-1] + (bits,))
    chosen = chosen.reshape(n_dev, n_dev, slots).transpose(1, 0, 2).reshape(n_dev, n_dev * slots)
    return chosen, slot


def select_body(field_ref, col_ref, cos_ref, sin_ref, out_ref, parts_ref):
    count, rows, nx = field_ref.shape
    planes = cos_ref.shape[1]
    points = col_ref.shape[2]
    flat = field_ref.reshape(count * rows, nx)
    for row in range(rows):
        value = flat[pl.ds(row, count, stride=rows), :]
        high = value.astype(BF16)
        low = (value - high.astype(F32)).astype(BF16)
        parts_ref[0:count, row * nx : (row + 1) * nx] = high
        parts_ref[count : 2 * count, row * nx : (row + 1) * nx] = low
    tile = min(points, 256)

    def step(index, carry):
        span = pl.ds(pl.multiple_of(index * tile, tile), tile)
        col = col_ref[0, :, span]
        place = lax.broadcasted_iota(jnp.int32, (rows * nx, tile), 0)
        hot = jnp.where(place == col, 1.0, 0.0).astype(BF16)
        both = jnp.dot(parts_ref[...], hot, preferred_element_type=F32)
        got = (both[:count] + both[count:]).reshape(2, count // (2 * planes), planes, tile)
        cosine, sine = cos_ref[0, :, span][None], sin_ref[0, :, span][None]
        real = jnp.sum(got[0] * cosine + got[1] * sine, axis=1)
        imag = jnp.sum(got[1] * cosine - got[0] * sine, axis=1)
        out_ref[0, :, span] = jnp.concatenate([real, imag], axis=0)
        return carry

    lax.fori_loop(0, points // tile, step, 0)


def select_sum(field, col, cos_z, sin_z):
    two, pairs, planes, ng, nx = field.shape
    groups, points = col.shape
    rows = ng // groups
    if rows % 8 == 0 and planes % 8 == 0 and nx % 128 == 0 and points % 256 == 0:
        count = two * pairs * planes
        flops = 4 * count * rows * nx * points * groups
        return pl.pallas_call(
            select_body,
            grid=(groups,),
            in_specs=[
                pl.BlockSpec((count, rows, nx), lambda g: (0, g, 0)),
                pl.BlockSpec((1, 1, points), lambda g: (g, 0, 0)),
                pl.BlockSpec((1, planes, points), lambda g: (g, 0, 0)),
                pl.BlockSpec((1, planes, points), lambda g: (g, 0, 0)),
            ],
            out_specs=pl.BlockSpec((1, 2 * pairs, points), lambda g: (g, 0, 0)),
            out_shape=jax.ShapeDtypeStruct((groups, 2 * pairs, points), F32),
            scratch_shapes=[pltpu.VMEM((2 * count, rows * nx), BF16)],
            cost_estimate=pl.CostEstimate(
                flops=flops, bytes_accessed=4 * count * ng * nx, transcendentals=0
            ),
        )(field.reshape(count, ng, nx), col[:, None, :], cos_z, sin_z)
    high, low = split(field.reshape(2, pairs, planes, groups, rows * nx))
    place = jnp.arange(rows * nx, dtype=jnp.int32)[None, :, None]
    hot = (place == col[:, None, :]).astype(BF16)
    form = "dpzsc,scq->sdpzq"
    got = jnp.einsum(form, high, hot, preferred_element_type=F32) + jnp.einsum(
        form, low, hot, preferred_element_type=F32
    )
    c, s = cos_z[:, None], sin_z[:, None]
    real = jnp.sum(got[:, 0] * c + got[:, 1] * s, axis=2)
    imag = jnp.sum(got[:, 1] * c - got[:, 0] * s, axis=2)
    return jnp.concatenate([real, imag], axis=1)


def halved(part, me, n_dev, bit):
    half = part.shape[2] // 2
    lower, upper = part[:, :, :half], part[:, :, half:]
    mine = me // (1 << bit) % 2 == 1
    route = [(k, k ^ (1 << bit)) for k in range(n_dev)]
    arrived = lax.ppermute(jnp.where(mine, lower, upper), "grid", route)
    return jnp.where(mine, upper, lower) + arrived


def summed_over_grid(part, me, n_dev, done):
    bits = n_dev.bit_length() - 1
    if n_dev == 1 << bits:
        for bit in range(done, bits):
            part = halved(part, me, n_dev, bit)
        return part
    groups, values, points = part.shape
    part = part.reshape(groups, values, n_dev, points // n_dev).transpose(2, 0, 1, 3)
    return lax.psum_scatter(part, "grid", scatter_dimension=0, tiled=False)


def local(left_bands, right_bands, sphere_index, right_order):
    n_dev = lax.axis_size("grid")
    me = lax.axis_index("grid")
    nl, zs, ng, nx = left_bands.shape[1:]
    own_right = right_bands.shape[1]
    rows = ng // n_dev
    other = swapped(right_bands, "band")
    chosen, slot = plan(sphere_index, ng, nx, n_dev)
    filled = chosen >= 0
    col = jnp.where(filled, chosen % (rows * nx), -1)
    kz = chosen // (rows * nx)
    plane = me * zs + jnp.arange(zs, dtype=jnp.int32)
    angle = (plane[None, :, None] * kz[:, None, :] % ng).astype(F32) * (2.0 * math.pi / ng)
    scale = 1.0 / (ng * ng * nx) ** 0.5
    cos_z, sin_z = jnp.cos(angle) * scale, jnp.sin(angle) * scale
    wx, wy = complex_matrix(nx), complex_matrix(ng)

    early = 2 if n_dev == 1 << (n_dev.bit_length() - 1) and n_dev >= 4 else 0

    def partial(right, beside):
        nr = right.shape[1]
        l0, l1 = left_bands[0][:, None], left_bands[1][:, None]
        r0, r1 = right[0][None], right[1][None]
        pair = jnp.stack([l0 * r0 + l1 * r1, l0 * r1 - l1 * r0])
        pair = pair.reshape(2, nl * nr, zs, ng, nx)
        pair = jnp.einsum("cpzyx,cxdk->dpzyk", pair, wx, precision=HIGH)
        if beside is not None and early:
            beside, pair = lax.optimization_barrier((halved(beside, me, n_dev, 0), pair))
        pair = jnp.einsum("cpzyk,cydq->dpzqk", pair, wy, precision=HIGH)
        if beside is not None and early:
            beside, pair = lax.optimization_barrier((halved(beside, me, n_dev, 1), pair))
        return select_sum(pair, col, cos_z, sin_z), beside

    first, _ = partial(right_bands, None)
    first, other = lax.optimization_barrier((first, other))
    second, first = partial(other, first)
    halves = []
    for part, done in ((first, early), (second, 0)):
        got = summed_over_grid(part, me, n_dev, done)
        got = got.transpose(1, 0, 2).reshape(2, nl, own_right, -1)
        halves.append(got)
    result = jnp.concatenate(halves, axis=2)
    own_slot = lax.dynamic_index_in_dim(slot, me, 0, keepdims=False)
    place = jnp.arange(result.shape[3], dtype=jnp.int32)
    pick = (place[:, None] == own_slot[None, :]).astype(F32)
    result = jnp.einsum("dnmt,ti->dnmi", result, pick, precision=HIGHEST)
    position = (right_order - lax.axis_index("band") * own_right) % right_order.shape[0]
    return jnp.take(result, position, axis=2)


def solution(mesh):
    placed = (P(None, "band", "grid", None, None), P(None, "band", "grid", None, None), P(), P())
    return jax.shard_map(
        local, mesh=mesh, in_specs=placed, out_specs=P(None, "band", None, "grid"), check_vma=False
    )
```

profile of v0, /device:TPU:0, one launch (start us, length us, event | category | flops | bytes accessed | tf_op | source)
XLA Modules:
  0.0 146.7 jit_solution(12738737332921467183)
XLA Ops:
  0.0 3.0 %collective-permute-start = (f32[2,2,8,128,128]{4,3,2,1,0:T(8,128)}, f32[2,2,8,128,128]{4,3,2,1,0:T(8,128)}, u32[]{:S(2)}, u32[]{:S(2)}) collective-permute-start(f32[2,2,8,128,128]{4,3,2,1,0:T(8,128)} %param.5), channel_id=1, source_target_pairs={{0,1},{1,0},{2,3},{3,2},{4,5},{5,4},{6,7},{7,6},{8,9},{9,8},{10,11... | collective-permute-start | bytes 6291464 | tf_op jit(solution)/shard_map/ppermute | solution.py:18
  3.0 2.7 %slice_bitcast_fusion.5 = (f32[2,8,128,128]{3,2,1,0:T(8,128)S(1)}, f32[2,8,128,128]{3,2,1,0:T(8,128)}) fusion(f32[2,2,8,128,128]{4,3,2,1,0:T(8,128)} %param.5), kind=kLoop, calls=%fused_computation.41 | loop fusion | bytes 4194304 | tf_op jit(solution)/shard_map/mul | solution.py:174
  5.7 0.9 fusion.62
  6.6 0.9 fusion.64
  7.5 0.0 copy-done.5
  7.5 0.2 fusion.47
  7.7 1.0 fusion.28
  8.7 8.8 %select_reduce_fusion = s32[16,1024]{1,0:T(8,128)S(1)} fusion(s32[16,1024]{1,0:T(8,128)S(1)} %add.209, s32[16,1024]{1,0:T(8,128)S(1)} %convert_add_fusion), kind=kLoop, calls=%fused_computation.1 | loop fusion | flops 50315264 | bytes 196608 | tf_op jit(solution)/shard_map/reduce_sum | solution.py:55
  17.6 0.1 copy.31
  17.7 0.1 reshape.354
  17.8 0.7 reshape.356
  18.6 0.1 reshape.355
  18.7 0.0 copy-start.2
  18.8 4.0 %slice_bitcast_fusion.1 = (f32[4,8,128,128]{3,2,1,0:T(8,128)S(1)}, f32[4,8,128,128]{3,2,1,0:T(8,128)}) fusion(f32[2,4,8,128,128]{4,3,2,1,0:T(8,128)} %param.4), kind=kLoop, calls=%fused_computation.29 | loop fusion | bytes 8388608 | tf_op jit(solution)/shard_map/mul | solution.py:174
  22.8 0.9 reshape.351
  23.7 1.1 copy.44
  24.7 1.5 %add_select_fusion.1 = s32[16,1024]{1,0:T(8,128)} fusion(s32[16,1024]{1,0:T(8,128)} %reshape.356), kind=kLoop, calls=%fused_computation.78 | loop fusion | flops 245760 | bytes 131072 | tf_op jit(solution)/shard_map/jit(floor_divide)/jit(_where)/select_n | solution.py:161
  26.3 4.1 %sine_multiply_fusion = (f32[16,8,1024]{2,1,0:T(8,128)}, f32[16,8,1024]{2,1,0:T(8,128)}) fusion(s32[16,1024]{1,0:T(8,128)} %add_select_fusion.1, s32[8]{0:T(128)S(1)} %iota_add_fusion.1), kind=kLoop, calls=%fused_computation.52 | loop fusion | flops 2097152 | bytes 1114144 | tf_op jit(solution)/shard_map/mul | solution.py:165
  30.4 3.1 %multiply_add_fusion.1 = (f32[4,2,8,128,128]{4,3,2,1,0:T(8,128)S(1)}, f32[4,2,8,128,128]{4,3,2,1,0:T(8,128)S(1)}) fusion(f32[2,8,128,128]{3,2,1,0:T(8,128)} %get-tuple-element.28, f32[4,8,128,128]{3,2,1,0:T(8,128)} %get-tuple-element.24, f32[2,8,128,128]{3,2,1,0:T(8,128)S(1)} %get-tuple-element.27, f32[4,8,128,128]{3,2,1,0:T(8,128)S(1)} %get-tuple-element.23), kind=kLoop, calls=%fused_computation.20 | loop fusion | flops 6291456 | bytes 14680064 | tf_op jit(solution)/shard_map/add | solution.py:174
  33.5 0.9 compare_select_fusion.2.col_ref
  34.3 4.6 %fusion = f32[2,128,8,8,128,1]{4,1,5,0,3,2:T(8,128)S(1)} fusion(f32[1,8,8,128,128]{4,3,0,2,1:T(8,128)S(1)} %bitcast.95, f32[1,8,8,128,128]{4,3,0,2,1:T(8,128)S(1)} %bitcast.94, f32[2,128,2,128,1,1]{1,3,0,5,4,2:T(8,128)S(1)} %copy.44), kind=kOutput, calls=%fused_computation.4 | convolution fusion | flops 3223322624 | bytes 17039360 | tf_op jit(solution)/shard_map/cpzyx,cxdk->dpzyk/dot_general | solution.py:176
  38.9 6.2 %fusion.6 = f32[2,128,8,8,128,1]{4,1,5,3,2,0:T(8,128)} fusion(f32[2,128,2,128,1,1]{1,3,0,5,4,2:T(8,128)S(1)} %copy.44, f32[2,128,8,8,128,1]{4,1,5,0,3,2:T(8,128)S(1)} %fusion), kind=kOutput, calls=%fused_computation.11 | convolution fusion | flops 3221225472 | bytes 17039360 | tf_op jit(solution)/shard_map/cpzyk,cydq->dpzqk/dot_general | solution.py:179
  45.2 26.0 %shard_map.46 = f32[16,16,1024]{2,1,0:T(8,128)} custom-call(f32[128,128,128]{2,1,0:T(8,128)} %bitcast.99, s32[16,1,1024]{2,1,0:T(1,128)} %compare_select_fusion.2.col_ref, f32[16,8,1024]{2,1,0:T(8,128)} %get-tuple-element.30.cos_ref, f32[16,8,1024]{2,1,0:T(8,128)} %get-tuple-element.29.sin_ref), custom_call_target="tpu_custom_call" | custom-call | flops 8589934592 | bytes 8388608 | tf_op jit(solution)/shard_map/pallas_call | solution.py:102
  71.2 0.0 collective-permute-done
  71.2 1.8 %slice_bitcast_fusion.3 = (f32[2,8,128,128]{3,2,1,0:T(8,128)S(1)}, f32[2,8,128,128]{3,2,1,0:T(8,128)S(1)}) fusion(f32[2,2,8,128,128]{4,3,2,1,0:T(8,128)} %collective-permute-done), kind=kLoop, calls=%fused_computation.35 | loop fusion | bytes 4194304 | tf_op jit(solution)/shard_map/mul | solution.py:174
  73.1 0.1 slice_select_fusion.1
  73.2 0.1 collective-permute-start.1
  73.2 0.5 copy-done
  73.8 1.5 %multiply_add_fusion = (f32[4,2,8,128,128]{4,3,2,1,0:T(8,128)S(1)}, f32[4,2,8,128,128]{4,3,2,1,0:T(8,128)S(1)}) fusion(f32[2,8,128,128]{3,2,1,0:T(8,128)S(1)} %get-tuple-element.26, f32[2,8,128,128]{3,2,1,0:T(8,128)S(1)} %get-tuple-element.25, f32[4,8,128,128]{3,2,1,0:T(8,128)S(1)} %copy-done, f32[4,8,128,128]{3,2,1,0:T(8,128)S(1)} %get-tuple-element.23), kind=kLoop, calls=%fused_computation.17 | loop fusion | flops 6291456 | bytes 14680064 | tf_op jit(solution)/shard_map/add | solution.py:174
  75.3 4.7 %fusion.17 = f32[2,8,8,128,128]{3,4,2,1,0:T(8,128)S(1)} fusion(f32[2,128,2,128,1,1]{1,3,0,5,4,2:T(8,128)S(1)} %copy.44, f32[1,8,8,128,128]{4,3,0,2,1:T(8,128)S(1)} %bitcast.97, f32[1,8,8,128,128]{4,3,0,2,1:T(8,128)S(1)} %bitcast.96), kind=kOutput, calls=%fused_computation.25 | convolution fusion | flops 3223322624 | bytes 17039360 | tf_op jit(solution)/shard_map/cpzyx,cxdk->dpzyk/dot_general | solution.py:176
  80.0 0.0 collective-permute-done.1
  80.0 0.1 select_add_fusion.1
  80.2 1.6 %collective-permute-start.2 = (f32[16,16,256]{2,1,0:T(8,128)S(1)}, f32[16,16,256]{2,1,0:T(8,128)S(1)}, u32[]{:S(2)}, u32[]{:S(2)}) collective-permute-start(f32[16,16,256]{2,1,0:T(8,128)S(1)} %slice_select_fusion.3), channel_id=1, source_target_pairs={{0,4},{2,6},{4,0},{6,2},{8,12},{10,14},{12,8},{14,10},{16,20},{18,... | collective-permute-start | bytes 786440 | tf_op jit(solution)/shard_map/ppermute | solution.py:136
  81.7 6.3 %fusion.14 = f32[2,8,8,128,128]{4,3,2,1,0:T(8,128)} fusion(f32[2,128,2,128,1,1]{1,3,0,5,4,2:T(8,128)S(1)} %copy.44, f32[2,8,8,128,128]{3,4,2,1,0:T(8,128)S(1)} %fusion.17), kind=kOutput, calls=%fused_computation.24 | convolution fusion | flops 3221225472 | bytes 17039360 | tf_op jit(solution)/shard_map/cpzyk,cydq->dpzqk/dot_general | solution.py:179
  88.1 0.4 collective-permute-done.2
  88.4 0.1 select_add_fusion.3
  88.5 0.0 copy-start.6
  88.5 26.1 %shard_map.47 = f32[16,16,1024]{2,1,0:T(8,128)} custom-call(f32[128,128,128]{2,1,0:T(8,128)} %bitcast.98, s32[16,1,1024]{2,1,0:T(1,128)} %compare_select_fusion.2.col_ref, f32[16,8,1024]{2,1,0:T(8,128)} %get-tuple-element.30.cos_ref, f32[16,8,1024]{2,1,0:T(8,128)} %get-tuple-element.29.sin_ref), custom_call_target="tpu_custom_call" | custom-call | flops 8589934592 | bytes 8388608 | tf_op jit(solution)/shard_map/pallas_call | solution.py:102
  114.6 1.3 slice_select_fusion
  115.9 0.1 collective-permute-start.5
  116.0 1.6 %collective-permute-start.3 = (f32[16,16,128]{2,1,0:T(8,128)S(1)}, f32[16,16,128]{2,1,0:T(8,128)S(1)}, u32[]{:S(2)}, u32[]{:S(2)}) collective-permute-start(f32[16,16,128]{2,1,0:T(8,128)S(1)} %slice_select_fusion.7), channel_id=1, source_target_pairs={{0,8},{2,10},{4,12},{6,14},{8,0},{10,2},{12,4},{14,6},{16,24},{18,... | collective-permute-start | bytes 393224 | tf_op jit(solution)/shard_map/ppermute | solution.py:136
  117.7 0.2 collective-permute-done.5
  117.8 1.4 select_add_fusion
  119.2 1.6 %collective-permute-start.6 = (f32[16,16,256]{2,1,0:T(8,128)S(1)}, f32[16,16,256]{2,1,0:T(8,128)S(1)}, u32[]{:S(2)}, u32[]{:S(2)}) collective-permute-start(f32[16,16,256]{2,1,0:T(8,128)S(1)} %slice_select_fusion.2), channel_id=1, source_target_pairs={{0,4},{2,6},{4,0},{6,2},{8,12},{10,14},{12,8},{14,10},{16,20},{18,... | collective-permute-start | bytes 786440 | tf_op jit(solution)/shard_map/ppermute | solution.py:136
  120.8 1.2 collective-permute-done.3
  122.0 5.7 %collective-permute-done.6 = f32[16,16,256]{2,1,0:T(8,128)S(1)} collective-permute-done((f32[16,16,256]{2,1,0:T(8,128)S(1)}, f32[16,16,256]{2,1,0:T(8,128)S(1)}, u32[]{:S(2)}, u32[]{:S(2)}) %collective-permute-start.6) | collective-permute-done | bytes 262176 | tf_op jit(solution)/shard_map/ppermute | solution.py:136
  127.7 0.1 select_add_fusion.2
  127.7 1.6 %collective-permute-start.7 = (f32[16,16,128]{2,1,0:T(8,128)S(1)}, f32[16,16,128]{2,1,0:T(8,128)S(1)}, u32[]{:S(2)}, u32[]{:S(2)}) collective-permute-start(f32[16,16,128]{2,1,0:T(8,128)S(1)} %slice_select_fusion.5), channel_id=1, source_target_pairs={{0,8},{2,10},{4,12},{6,14},{8,0},{10,2},{12,4},{14,6},{16,24},{18,... | collective-permute-start | bytes 393224 | tf_op jit(solution)/shard_map/ppermute | solution.py:136
  129.4 0.1 slice_select_fusion.6
  129.5 2.7 %collective-permute-start.4 = (f32[16,16,64]{2,1,0:T(8,128)S(1)}, f32[16,16,64]{2,1,0:T(8,128)S(1)}, u32[]{:S(2)}, u32[]{:S(2)}) collective-permute-start(f32[16,16,64]{2,1,0:T(8,128)S(1)} %slice_select_fusion.6), channel_id=1, source_target_pairs={{0,16},{2,18},{4,20},{6,22},{8,24},{10,26},{12,28},{14,30},{16,0},... | collective-permute-start | bytes 196616 | tf_op jit(solution)/shard_map/ppermute | solution.py:136
  132.1 2.1 %collective-permute-done.7 = f32[16,16,128]{2,1,0:T(8,128)S(1)} collective-permute-done((f32[16,16,128]{2,1,0:T(8,128)S(1)}, f32[16,16,128]{2,1,0:T(8,128)S(1)}, u32[]{:S(2)}, u32[]{:S(2)}) %collective-permute-start.7) | collective-permute-done | bytes 131104 | tf_op jit(solution)/shard_map/ppermute | solution.py:136
  134.2 0.1 slice_select_fusion.4
  134.3 2.3 %collective-permute-start.8 = (f32[16,16,64]{2,1,0:T(8,128)S(1)}, f32[16,16,64]{2,1,0:T(8,128)S(1)}, u32[]{:S(2)}, u32[]{:S(2)}) collective-permute-start(f32[16,16,64]{2,1,0:T(8,128)S(1)} %slice_select_fusion.4), channel_id=1, source_target_pairs={{0,16},{2,18},{4,20},{6,22},{8,24},{10,26},{12,28},{14,30},{16,0},... | collective-permute-start | bytes 196616 | tf_op jit(solution)/shard_map/ppermute | solution.py:136
  136.7 5.0 %collective-permute-done.4 = f32[16,16,64]{2,1,0:T(8,128)S(1)} collective-permute-done((f32[16,16,64]{2,1,0:T(8,128)S(1)}, f32[16,16,64]{2,1,0:T(8,128)S(1)}, u32[]{:S(2)}, u32[]{:S(2)}) %collective-permute-start.4) | collective-permute-done | bytes 65568 | tf_op jit(solution)/shard_map/ppermute | solution.py:136
  141.7 0.1 add_bitcast_fusion.1
  141.8 0.1 reshape.357
  142.0 1.4 collective-permute-done.8
  143.3 0.1 add_bitcast_fusion
  143.5 0.1 reshape.359
  143.6 0.1 pad_maximum_fusion
  143.7 1.6 %fusion.12 = f32[2,4,4,1024]{3,1,2,0:T(4,128)S(1)} fusion(s32[1024]{0:T(1024)S(1)} %bitcast.103, f32[2,4,4,1024]{3,2,1,0:T(4,128)S(1)} %pad_maximum_fusion), kind=kOutput, calls=%fused_computation.23 | convolution fusion | flops 403701760 | bytes 266240 | tf_op jit(solution)/shard_map/dnmt,ti->dnmi/dot_general | solution.py:196
  145.3 0.6 gather_fusion
  145.9 0.1 select_bitcast_fusion
  146.0 0.7 copy.40
  (30 shorter events, 0.5 us)
Async XLA Ops:
  0.0 7.5 %copy-start.5 = (s32[16384]{0:T(1024)S(1)}, s32[16384]{0:T(1024)}, u32[]{:S(2)}) copy-start(s32[16384]{0:T(1024)} %param.6) | copy-start | bytes 196612
  0.0 71.2 %collective-permute-start = (f32[2,2,8,128,128]{4,3,2,1,0:T(8,128)}, f32[2,2,8,128,128]{4,3,2,1,0:T(8,128)}, u32[]{:S(2)}, u32[]{:S(2)}) collective-permute-start(f32[2,2,8,128,128]{4,3,2,1,0:T(8,128)} %param.5), channel_id=1, source_target_pairs={{0,1},{1,0},{2,3},{3,2},{4,5},{5,4},{6,7},{7,6},{8,9},{9,8},{10,11... | collective-permute-start | bytes 6291464 | tf_op jit(solution)/shard_map/ppermute | solution.py:18
  18.7 4.0 %copy-start.2 = (f32[128,128]{1,0:T(8,128)S(1)}, f32[128,128]{1,0:T(8,128)}, u32[]{:S(2)}) copy-start(f32[128,128]{1,0:T(8,128)} %get-tuple-element.33) | copy-start | bytes 196612
  18.8 4.0 %copy-start.3 = (f32[128,128]{1,0:T(8,128)S(1)}, f32[128,128]{1,0:T(8,128)}, u32[]{:S(2)}) copy-start(f32[128,128]{1,0:T(8,128)} %get-tuple-element.34) | copy-start | bytes 196612
  18.8 4.0 %copy-start.4 = (f32[128,128]{1,0:T(8,128)S(1)}, f32[128,128]{1,0:T(8,128)}, u32[]{:S(2)}) copy-start(f32[128,128]{1,0:T(8,128)} %fusion.64) | copy-start | bytes 196612
  71.2 1.9 %copy-start.1 = (f32[16,16,1024]{2,1,0:T(8,128)S(1)}, f32[16,16,1024]{2,1,0:T(8,128)}, u32[]{:S(2)}) copy-start(f32[16,16,1024]{2,1,0:T(8,128)} %shard_map.46) | copy-start | bytes 3145732
  71.2 2.5 %copy-start = (f32[4,8,128,128]{3,2,1,0:T(8,128)S(1)}, f32[4,8,128,128]{3,2,1,0:T(8,128)}, u32[]{:S(2)}) copy-start(f32[4,8,128,128]{3,2,1,0:T(8,128)} %get-tuple-element.24) | copy-start | bytes 6291460
  73.2 6.8 %collective-permute-start.1 = (f32[16,16,512]{2,1,0:T(8,128)S(1)}, f32[16,16,512]{2,1,0:T(8,128)S(1)}, u32[]{:S(2)}, u32[]{:S(2)}) collective-permute-start(f32[16,16,512]{2,1,0:T(8,128)S(1)} %slice_select_fusion.1), channel_id=1, source_target_pairs={{0,2},{2,0},{4,6},{6,4},{8,10},{10,8},{12,14},{14,12},{16,18},{18,... | collective-permute-start | bytes 1572872 | tf_op jit(solution)/shard_map/ppermute | solution.py:136
  80.2 8.3 %collective-permute-start.2 = (f32[16,16,256]{2,1,0:T(8,128)S(1)}, f32[16,16,256]{2,1,0:T(8,128)S(1)}, u32[]{:S(2)}, u32[]{:S(2)}) collective-permute-start(f32[16,16,256]{2,1,0:T(8,128)S(1)} %slice_select_fusion.3), channel_id=1, source_target_pairs={{0,4},{2,6},{4,0},{6,2},{8,12},{10,14},{12,8},{14,10},{16,20},{18,... | collective-permute-start | bytes 786440 | tf_op jit(solution)/shard_map/ppermute | solution.py:136
  88.5 27.5 %copy-start.6 = (s32[4]{0:T(128)S(1)}, s32[4]{0:T(128)}, u32[]{:S(2)}) copy-start(s32[4]{0:T(128)} %param.7) | copy-start | bytes 52
  115.9 2.0 %collective-permute-start.5 = (f32[16,16,512]{2,1,0:T(8,128)S(1)}, f32[16,16,512]{2,1,0:T(8,128)S(1)}, u32[]{:S(2)}, u32[]{:S(2)}) collective-permute-start(f32[16,16,512]{2,1,0:T(8,128)S(1)} %slice_select_fusion), channel_id=1, source_target_pairs={{0,2},{2,0},{4,6},{6,4},{8,10},{10,8},{12,14},{14,12},{16,18},{18,... | collective-permute-start | bytes 1572872 | tf_op jit(solution)/shard_map/ppermute | solution.py:136
  116.0 5.9 %collective-permute-start.3 = (f32[16,16,128]{2,1,0:T(8,128)S(1)}, f32[16,16,128]{2,1,0:T(8,128)S(1)}, u32[]{:S(2)}, u32[]{:S(2)}) collective-permute-start(f32[16,16,128]{2,1,0:T(8,128)S(1)} %slice_select_fusion.7), channel_id=1, source_target_pairs={{0,8},{2,10},{4,12},{6,14},{8,0},{10,2},{12,4},{14,6},{16,24},{18,... | collective-permute-start | bytes 393224 | tf_op jit(solution)/shard_map/ppermute | solution.py:136
  119.2 8.4 %collective-permute-start.6 = (f32[16,16,256]{2,1,0:T(8,128)S(1)}, f32[16,16,256]{2,1,0:T(8,128)S(1)}, u32[]{:S(2)}, u32[]{:S(2)}) collective-permute-start(f32[16,16,256]{2,1,0:T(8,128)S(1)} %slice_select_fusion.2), channel_id=1, source_target_pairs={{0,4},{2,6},{4,0},{6,2},{8,12},{10,14},{12,8},{14,10},{16,20},{18,... | collective-permute-start | bytes 786440 | tf_op jit(solution)/shard_map/ppermute | solution.py:136
  127.7 6.5 %collective-permute-start.7 = (f32[16,16,128]{2,1,0:T(8,128)S(1)}, f32[16,16,128]{2,1,0:T(8,128)S(1)}, u32[]{:S(2)}, u32[]{:S(2)}) collective-permute-start(f32[16,16,128]{2,1,0:T(8,128)S(1)} %slice_select_fusion.5), channel_id=1, source_target_pairs={{0,8},{2,10},{4,12},{6,14},{8,0},{10,2},{12,4},{14,6},{16,24},{18,... | collective-permute-start | bytes 393224 | tf_op jit(solution)/shard_map/ppermute | solution.py:136
  129.5 12.2 %collective-permute-start.4 = (f32[16,16,64]{2,1,0:T(8,128)S(1)}, f32[16,16,64]{2,1,0:T(8,128)S(1)}, u32[]{:S(2)}, u32[]{:S(2)}) collective-permute-start(f32[16,16,64]{2,1,0:T(8,128)S(1)} %slice_select_fusion.6), channel_id=1, source_target_pairs={{0,16},{2,18},{4,20},{6,22},{8,24},{10,26},{12,28},{14,30},{16,0},... | collective-permute-start | bytes 196616 | tf_op jit(solution)/shard_map/ppermute | solution.py:136
  134.3 9.0 %collective-permute-start.8 = (f32[16,16,64]{2,1,0:T(8,128)S(1)}, f32[16,16,64]{2,1,0:T(8,128)S(1)}, u32[]{:S(2)}, u32[]{:S(2)}) collective-permute-start(f32[16,16,64]{2,1,0:T(8,128)S(1)} %slice_select_fusion.4), channel_id=1, source_target_pairs={{0,16},{2,18},{4,20},{6,22},{8,24},{10,26},{12,28},{14,30},{16,0},... | collective-permute-start | bytes 196616 | tf_op jit(solution)/shard_map/ppermute | solution.py:136
where the time goes:
time: 147 us
  Pallas kernels  52.1 us (35%)
  other arithmetic  25.5 us (17%)
  matrix products  24.5 us (17%)
  waiting for transfers between devices  15.9 us (11%)
  starting transfers between devices  14.5 us (10%)
  local copies, waits for them, and re-layouts  13.8 us (9%)
    pallas_call x2, Pallas kernels, select_sum(): pl.pallas_call(select_body, grid=(groups,), in_specs=[pl.BlockSpec((count...  52.1 us
    ppermute x8, waiting for transfers between devices, halved(): arrived = lax.ppermute(jnp.where(mine, lower, upper), 'grid', route)  15.9 us
    dot_general x2, matrix products, partial(): pair = jnp.einsum('cpzyk,cydq->dpzqk', pair, wy, precision=HIGH)  12.6 us
    ppermute x8, starting transfers between devices, halved(): arrived = lax.ppermute(jnp.where(mine, lower, upper), 'grid', route)  11.5 us
    dot_general x2, matrix products, partial(): pair = jnp.einsum('cpzyx,cxdk->dpzyk', pair, wx, precision=HIGH)  9.31 us
    reduce_sum x1, other arithmetic, plan(): jnp.sum(jnp.where(slot[:, :, None] == target[None, None, :], packed[:, :,...  8.79 us
    mul x3, local copies, waits for them, and re-layouts, partial(): pair = jnp.stack([l0 * r0 + l1 * r1, l0 * r1 - l1 * r0])  8.53 us
    add x2, other arithmetic, partial(): pair = jnp.stack([l0 * r0 + l1 * r1, l0 * r1 - l1 * r0])  4.58 us
  transfers between devices with their start and end apart: 9, of which 7 were waited for; matrix products, arithmetic and copies ran while one was open for 38% of the time, Pallas kernels for 18%

commit v1 on v0

--- a/solution.py
+++ b/solution.py
@@ -2,6 +2,7 @@
 
 import jax
 import jax.numpy as jnp
+import numpy as np
 from jax import lax
 from jax.experimental import pallas as pl
 from jax.experimental.pallas import tpu as pltpu
@@ -148,8 +149,439 @@
     return lax.psum_scatter(part, "grid", scatter_dimension=0, tiled=False)
 
 
+LANES = 128
+SUBLANES = 8
+MESH = pl.DeviceIdType.MESH
+
+
+def constant_matrix(length):
+    counter = np.arange(length)
+    angles = (counter[:, None] * counter[None, :] % length) * (2.0 * math.pi / length)
+    cosine, sine = np.cos(angles), np.sin(angles)
+    return np.concatenate(
+        [np.concatenate([cosine, -sine], 1), np.concatenate([sine, cosine], 1)], 0
+    ).astype(np.float32)
+
+
+def constant_split(value):
+    high = value.astype(BF16)
+    return high, (value - high.astype(np.float32)).astype(BF16)
+
+
+def dot(a, b):
+    return jnp.dot(a, b, preferred_element_type=F32)
+
+
+def parts(value):
+    high = value.astype(BF16)
+    return high, (value - high.astype(F32)).astype(BF16)
+
+
+def lane_gather(value, index):
+    return jnp.take_along_axis(value, index, axis=1, mode="promise_in_bounds")
+
+
+def fused_body(
+    n_dev,
+    left_hbm, right_hbm, index_ref, pos_ref, upper_ref, table_ref, wyh, wyl, wxh, wxl,
+    out_ref,
+    left, right, field, acc, came, came2, final, plan_kx, plan_ky, cos_z, sin_z, own_slot,
+    sem_in, sem_xs, sem_xr, sem_1s, sem_1r, sem_2s, sem_2r, sem_3s, sem_3r,
+):
+    nl, planes, ng, nx = left.shape[1:]
+    own = right_hbm.shape[1]
+    nr = right.shape[1]
+    rows = ng // n_dev
+    chips = n_dev // 2
+    pitch = field.shape[2] // (2 * nl)
+    slots = LANES // 2
+    blocks = index_ref.shape[0] // n_dev
+    spans = sem_xs.shape[0] // own
+    step = planes // spans
+    me = lax.axis_index("grid")
+    band = lax.axis_index("band")
+    core, chip = lax.rem(me, 2), me // 2
+    partner = me + 1 - 2 * core
+
+    def at(grid):
+        return {"grid": grid, "band": band}
+
+    barrier = pltpu.get_barrier_semaphore()
+    pl.semaphore_signal(
+        barrier, inc=1, device_id={"grid": me, "band": 1 - band}, device_id_type=MESH
+    )
+    pl.semaphore_signal(barrier, inc=1, device_id=at(partner), device_id_type=MESH)
+    for o in range(1, chips):
+        other = lax.rem(chip + o, chips) * 2 + core
+        pl.semaphore_signal(barrier, inc=1, device_id=at(other), device_id_type=MESH)
+    load_right = pltpu.make_async_copy(right_hbm, right.at[:, 0:own], sem_in.at[0])
+    load_left = pltpu.make_async_copy(left_hbm, left, sem_in.at[1])
+    load_right.start()
+    load_left.start()
+    pl.semaphore_wait(barrier, chips + 1)
+
+    def remote(src, dst, send, recv, where):
+        return pltpu.make_async_remote_copy(
+            src_ref=src, dst_ref=dst, send_sem=send, recv_sem=recv,
+            device_id=where, device_id_type=MESH,
+        )
+
+    def swap(m, span):
+        part = pl.ds(span * step, step)
+        k = m * spans + span
+        return remote(
+            right_hbm.at[:, m, part], right.at[:, own + m, part],
+            sem_xs.at[k], sem_xr.at[k], {"grid": me, "band": 1 - band},
+        )
+
+    for m in range(own):
+        for span in range(spans):
+            swap(m, span).start()
+
+    bit_x, bit_y = nx.bit_length() - 1, ng.bit_length() - 1
+    bit_r = rows.bit_length() - 1
+    iota_s = lax.broadcasted_iota(jnp.int32, (n_dev, LANES), 0)
+    iota_r = lax.broadcasted_iota(jnp.int32, (slots, LANES), 0)
+    iota_p = lax.broadcasted_iota(jnp.int32, (planes, LANES), 0)
+
+    def plan_block(t):
+        value = index_ref[pl.ds(pl.multiple_of(t * blocks, blocks), blocks), :]
+        source = (value >> (bit_x + bit_r)) & (n_dev - 1)
+        ky = (value >> bit_x) & (rows - 1)
+        kx = value & (nx - 1)
+        kz = value >> (bit_x + bit_y)
+        masks = [
+            jnp.broadcast_to(source[c : c + 1], (n_dev, LANES)) == iota_s for c in range(blocks)
+        ]
+        hot = jnp.concatenate([jnp.where(k, 1.0, 0.0) for k in masks], 0).astype(BF16)
+        prefix = dot(hot, upper_ref[...])
+        carry = jnp.zeros((n_dev, LANES), F32)
+        left_side, right_side, ranks = [], [], []
+        for c in range(blocks):
+            mine = prefix[c * n_dev : (c + 1) * n_dev]
+            count = mine[:, :LANES] + carry
+            carry = carry + mine[:, LANES:]
+            rank = jnp.sum(jnp.where(masks[c], count, 0.0), axis=0, keepdims=True)
+            rank = rank.astype(jnp.int32)
+            ranks.append(rank)
+            wide = [
+                jnp.where(
+                    masks[c],
+                    jnp.broadcast_to(v[c : c + 1].astype(F32), (n_dev, LANES)), 0.0
+                )
+                for v in (kz, ky, kx)
+            ]
+            left_side.append(jnp.concatenate(wide, 0))
+            right_side.append(
+                jnp.where(jnp.broadcast_to(rank, (slots, LANES)) == iota_r, 1.0, 0.0)
+            )
+        own_slot[t, 0] = source
+        own_slot[t, 1] = jnp.concatenate(ranks, 0)
+        a = jnp.concatenate(left_side, 1).astype(BF16)
+        b = jnp.concatenate(right_side, 1).astype(BF16)
+        return lax.dot_general(a, b, (((1,), (1,)), ((), ())), preferred_element_type=F32)
+
+    def plan_chip(ch, carry):
+        both = jnp.concatenate([plan_block(2 * ch), plan_block(2 * ch + 1)], 1)
+        both = both.astype(jnp.int32)
+        kz = both[0:n_dev]
+        plan_ky[ch] = both[n_dev : 2 * n_dev]
+        plan_kx[ch] = both[2 * n_dev : 3 * n_dev]
+        for g in range(n_dev):
+            turn = jnp.broadcast_to(kz[g : g + 1], (planes, LANES)) * (me * planes + iota_p)
+            turn = turn & (ng - 1)
+            cos_z[ch, g] = lane_gather(table_ref[0], turn)
+            sin_z[ch, g] = lane_gather(table_ref[1], turn)
+        return carry
+
+    lax.fori_loop(0, chips, plan_chip, 0)
+
+    def transform(m, z, q, buf):
+        r0, r1 = right[0, m, z], right[1, m, z]
+        real, imag = [], []
+        for e in range(2):
+            l0, l1 = left[0, 2 * q + e, z], left[1, 2 * q + e, z]
+            real.append(l0 * r0 + l1 * r1)
+            imag.append(l0 * r1 - l1 * r0)
+        pair = jnp.concatenate([jnp.concatenate(real, 1), jnp.concatenate(imag, 1)], 0)
+        high, low = parts(pair)
+        y = dot(wyh[...], high) + dot(wyl[...], high) + dot(wyh[...], low)
+        lines = jnp.concatenate(
+            [
+                jnp.concatenate([y[:ng, e * nx : (e + 1) * nx], y[ng:, e * nx : (e + 1) * nx]], 1)
+                for e in range(2)
+            ],
+            0,
+        )
+        high, low = parts(lines)
+        x = dot(high, wxh[...]) + dot(low, wxh[...]) + dot(high, wxl[...])
+        for d in range(2):
+            for e in range(2):
+                start = pl.multiple_of((d * nl + 2 * q + e) * pitch, SUBLANES)
+                field[buf, z, pl.ds(start, ng), :] = x[
+                    e * ng : (e + 1) * ng, d * nx : (d + 1) * nx
+                ]
+
+    sign = jnp.where(lax.broadcasted_iota(jnp.int32, (2 * nl, LANES), 0) < nl, 1.0, -1.0)
+
+    def choose(items, bits):
+        for bit in bits:
+            items = [jnp.where(bit, items[2 * k + 1], items[2 * k]) for k in range(len(items) // 2)]
+        return items[0]
+
+    def bits_of(value, count, shape):
+        value = jnp.broadcast_to(value, shape)
+        return [((value >> i) & 1) == 1 for i in range(count)]
+
+    def gather_group(m, g, buf, zs, add):
+        half, inner = g // (n_dev // 2), lax.rem(g, n_dev // 2)
+        shape = (2 * nl, LANES)
+        for ch in range(chips):
+            index = jnp.broadcast_to(plan_kx[ch, pl.ds(g, 1), :], shape)
+            bits = bits_of(plan_ky[ch, pl.ds(g, 1), :], bit_r, shape)
+            even = odd = None
+            for z in zs:
+                got = choose(
+                    [
+                        lane_gather(
+                            field[buf, z, pl.ds(g * rows + k, 2 * nl, stride=pitch), :], index
+                        )
+                        for k in range(rows)
+                    ],
+                    bits,
+                )
+                c = jnp.broadcast_to(cos_z[ch, g, pl.ds(z, 1), :], shape)
+                s = jnp.broadcast_to(sin_z[ch, g, pl.ds(z, 1), :], shape)
+                even = got * c if even is None else even + got * c
+                odd = got * s if odd is None else odd + got * s
+            total = even + sign * pltpu.roll(odd, nl, 0)
+            if add:
+                total = total + acc[m, half, ch, inner]
+            acc[m, half, ch, inner] = total
+
+    def send1(m):
+        return remote(
+            acc.at[m, 1 - core], came.at[m], sem_1s.at[m], sem_1r.at[m], at(partner)
+        )
+
+    def send2(m, o):
+        other = lax.rem(chip + o, chips)
+        return remote(
+            acc.at[m, core, other], came2.at[m, o - 1],
+            sem_2s.at[m, o - 1], sem_2r.at[m, o - 1], at(other * 2 + core),
+        )
+
+    def send3(m):
+        return remote(
+            final.at[m, core], final.at[m, core], sem_3s.at[m], sem_3r.at[m], at(partner)
+        )
+
+    def stage2(m):
+        send1(m).wait_recv()
+
+        def add(ch, carry):
+            acc[m, core, ch] = acc[m, core, ch] + came[m, ch]
+            return carry
+
+        lax.fori_loop(0, chips, add, 0)
+        for o in range(1, chips):
+            send2(m, o).start()
+
+    def stage3(m):
+        for o in range(1, chips):
+            send2(m, o).wait_recv()
+        total = acc[m, core, chip]
+        for o in range(1, chips):
+            total = total + came2[m, o - 1]
+        final[m, core] = total
+        send3(m).start()
+
+    load_right.wait()
+    load_left.wait()
+    half = nl // 2
+
+    def first(z, carry):
+        for q in range(half):
+            transform(0, z, q, 0)
+        return carry
+
+    lax.fori_loop(0, planes, first, 0)
+
+    def both(m, buf):
+        def run(g, carry):
+            gather_group(m, g, buf, range(planes), False)
+            transform(m + 1, g // half, lax.rem(g, half), 1 - buf)
+            return carry
+
+        lax.fori_loop(0, n_dev, run, 0)
+
+    def only(m, buf):
+        def run(g, carry):
+            gather_group(m, g, buf, range(planes), False)
+            return carry
+
+        lax.fori_loop(0, n_dev, run, 0)
+
+    both(0, 0)
+    send1(0).start()
+    for span in range(spans):
+        swap(0, span).wait_recv()
+    both(1, 1)
+    send1(1).start()
+    stage2(0)
+    only(2, 0)
+    send1(2).start()
+    stage2(1)
+    stage3(0)
+
+    def clear(i, carry):
+        acc[3, i // chips, lax.rem(i, chips)] = jnp.zeros(acc.shape[3:], F32)
+        return carry
+
+    lax.fori_loop(0, 2 * chips, clear, 0)
+
+    def tail(span, carry):
+        swap(1, span).wait_recv()
+
+        def work(k, carry):
+            for q in range(half):
+                transform(3, span * step + k, q, 1)
+            return carry
+
+        lax.fori_loop(0, step, work, 0)
+
+        def run(k, carry):
+            for e in range(4):
+                gather_group(
+                    3, k * 4 + e, 1, [span * step + z for z in range(step)], True
+                )
+            return carry
+
+        lax.fori_loop(0, n_dev // 4, run, 0)
+        return carry
+
+    lax.fori_loop(0, spans, tail, 0)
+    send1(3).start()
+    stage2(2)
+    stage3(1)
+    stage2(3)
+    stage3(2)
+    stage3(3)
+    for m in range(nr):
+        send3(m).wait_recv()
+
+    source, rank = own_slot[me, 0], own_slot[me, 1]
+    shape = (2 * nl, LANES)
+    for c in range(blocks):
+        index = jnp.broadcast_to(rank[c : c + 1] + core * slots, shape)
+        bits = bits_of(source[c : c + 1], n_dev.bit_length() - 1, shape)
+        got = [
+            choose(
+                [
+                    lane_gather(final[m, g // chips, g % chips], index)
+                    for g in range(n_dev)
+                ],
+                bits,
+            )
+            for m in range(nr)
+        ]
+        for j in range(nr):
+            pos = jnp.broadcast_to(pos_ref[j : j + 1, :], shape)
+            value = got[0]
+            for m in range(1, nr):
+                value = jnp.where(pos == m, got[m], value)
+            out_ref[j, :, c * LANES : (c + 1) * LANES] = value
+
+    for m in range(own):
+        for span in range(spans):
+            swap(m, span).wait_send()
+    for m in range(nr):
+        send1(m).wait_send()
+        for o in range(1, chips):
+            send2(m, o).wait_send()
+        send3(m).wait_send()
+
+
+def fused_fits(left_bands, right_bands, sphere_index, n_dev):
+    two, nl, zs, ng, nx = left_bands.shape
+    per = sphere_index.shape[0] // n_dev
+    return (
+        ng == nx == LANES
+        and zs * n_dev == ng
+        and zs == SUBLANES
+        and 2 * nl == SUBLANES
+        and right_bands.shape[1] == 2
+        and lax.axis_size("band") == 2
+        and per == SUBLANES * LANES
+        and 2 * (per // n_dev) == LANES
+        and n_dev == 2 * SUBLANES
+    )
+
+
+def fused(left_bands, right_bands, sphere_index, right_order):
+    n_dev = lax.axis_size("grid")
+    two, nl, zs, ng, nx = left_bands.shape
+    own = right_bands.shape[1]
+    nr = right_order.shape[0]
+    chips = n_dev // 2
+    per = sphere_index.shape[0] // n_dev
+    spans = 4
+    pitch = ng + SUBLANES
+    scale = 1.0 / (ng * ng * nx) ** 0.5
+    position = (right_order - lax.axis_index("band") * own) % nr
+    position = jnp.broadcast_to(position.astype(jnp.int32)[:, None], (nr, LANES))
+    upper = np.concatenate([np.triu(np.ones((LANES, LANES)), 1), np.ones((LANES, LANES))], 1)
+    angle = np.arange(ng) * (2.0 * math.pi / ng)
+    table = np.stack([np.cos(angle), np.sin(angle)]) * scale
+    table = np.broadcast_to(table[:, None], (2, SUBLANES, ng)).astype(np.float32)
+    wyh, wyl = constant_split(np.ascontiguousarray(constant_matrix(ng).T))
+    wxh, wxl = constant_split(constant_matrix(nx))
+    constants = [upper.astype(BF16), table, wyh, wyl, wxh, wxl]
+    vmem = pl.BlockSpec(memory_space=pltpu.VMEM)
+    anywhere = pl.BlockSpec(memory_space=pl.ANY)
+    dma = pltpu.SemaphoreType.DMA
+    result = pl.pallas_call(
+        lambda *refs: fused_body(n_dev, *refs),
+        in_specs=[anywhere, anywhere] + [vmem] * 8,
+        out_specs=vmem,
+        out_shape=jax.ShapeDtypeStruct((nr, 2 * nl, per), F32),
+        scratch_shapes=[
+            pltpu.VMEM((two, nl, zs, ng, nx), F32),
+            pltpu.VMEM((two, nr, zs, ng, nx), F32),
+            pltpu.VMEM((2, zs, 2 * nl * pitch, nx), F32),
+            pltpu.VMEM((nr, 2, chips, n_dev // 2, 2 * nl, LANES), F32),
+            pltpu.VMEM((nr, chips, n_dev // 2, 2 * nl, LANES), F32),
+            pltpu.VMEM((nr, chips - 1, n_dev // 2, 2 * nl, LANES), F32),
+            pltpu.VMEM((nr, 2, n_dev // 2, 2 * nl, LANES), F32),
+            pltpu.VMEM((chips, n_dev, LANES), jnp.int32),
+            pltpu.VMEM((chips, n_dev, LANES), jnp.int32),
+            pltpu.VMEM((chips, n_dev, zs, LANES), F32),
+            pltpu.VMEM((chips, n_dev, zs, LANES), F32),
+            pltpu.VMEM((n_dev, 2, per // LANES, LANES), jnp.int32),
+            dma((2,)),
+            dma((own * spans,)),
+            dma((own * spans,)),
+            dma((nr,)),
+            dma((nr,)),
+            dma((nr, chips - 1)),
+            dma((nr, chips - 1)),
+            dma((nr,)),
+            dma((nr,)),
+        ],
+        compiler_params=pltpu.CompilerParams(
+            collective_id=0, has_side_effects=True, vmem_limit_bytes=60 * 1024 * 1024
+        ),
+    )(
+        left_bands, right_bands, sphere_index.reshape(-1, LANES), position,
+        *[jnp.asarray(c) for c in constants],
+    )
+    return result.transpose(1, 0, 2).reshape(2, nl, nr, per)
+
+
 def local(left_bands, right_bands, sphere_index, right_order):
     n_dev = lax.axis_size("grid")
+    if fused_fits(left_bands, right_bands, sphere_index, n_dev):
+        return fused(left_bands, right_bands, sphere_index, right_order)
     me = lax.axis_index("grid")
     nl, zs, ng, nx = left_bands.shape[1:]
     own_right = right_bands.shape[1]

time: 147 us -> 88.7 us (0.60)
  Pallas kernels: 52.1 us -> 85 us
  other arithmetic: 25.5 us -> 0.66 us
  matrix products: 24.5 us -> 0 us
  waiting for transfers between devices: 15.9 us -> 0 us
  starting transfers between devices: 14.5 us -> 0 us
  local copies, waits for them, and re-layouts: 13.8 us -> 2.29 us
    pallas_call x2 -> x1, Pallas kernels: 52.1 us -> 85 us  [fused(): pl.pallas_call(lambda *refs: fused_body(n_dev, *refs), in_specs=[anywhere...]
    dot_general x6 -> x0, matrix products: 24.5 us -> none  [the longest x2 12.6 us: partial(): pair = jnp.einsum('cpzyk,cydq->dpzqk', pair, wy, precision=HIGH)]
    ppermute x9 -> x0, waiting for transfers between devices: 15.9 us -> none  [the longest x8 15.9 us: halved(): arrived = lax.ppermute(jnp.where(mine, lower, upper), 'grid', route)]
    ppermute x9 -> x0, starting transfers between devices: 14.5 us -> none  [the longest x8 11.5 us: halved(): arrived = lax.ppermute(jnp.where(mine, lower, upper), 'grid', route)]
    reduce_sum x1 -> x0, other arithmetic: 8.79 us -> none  [plan(): jnp.sum(jnp.where(slot[:, :, None] == target[None, None, :], packed[:, :,...]
    mul x3 -> x0, local copies, waits for them, and re-layouts: 8.53 us -> none  [partial(): pair = jnp.stack([l0 * r0 + l1 * r1, l0 * r1 - l1 * r0])]
    add x12 -> x0, other arithmetic: 6.43 us -> none  [the longest x2 4.58 us: partial(): pair = jnp.stack([l0 * r0 + l1 * r1, l0 * r1 - l1 * r0])]
    mul x1 -> x0, other arithmetic: 4.1 us -> none  [local(): cos_z, sin_z = (jnp.cos(angle) * scale, jnp.sin(angle) * scale)]
  transfers between devices with their start and end apart: 9 -> 0, of which waited for: 7 -> 0; matrix products, arithmetic and copies ran while one was open for 38% -> 0% of each run, Pallas kernels for 18% -> 0%
where the time goes in v1:
time: 88.7 us; the launch traced here: 88 us
  Pallas kernels  85 us (96%)
  local copies, waits for them, and re-layouts  2.29 us (3%)
    pallas_call x1, Pallas kernels, fused(): pl.pallas_call(lambda *refs: fused_body(n_dev, *refs), in_specs=[anywhere...  85 us

profile of v1, /device:TPU:0, one launch (start us, length us, event | category | flops | bytes accessed | tf_op | source)
XLA Modules:
  0.0 88.0 jit_solution(17319457794596877701)
XLA Ops:
  0.0 0.7 and_select_fusion
  0.7 0.6 broadcast_in_dim.2.refs_3_
  1.3 85.0 %shard_map.100 = f32[4,8,1024]{2,1,0:T(8,128)} custom-call(f32[2,4,8,128,128]{4,3,2,1,0:T(8,128)} %refs_0_.1, f32[2,2,8,128,128]{4,3,2,1,0:T(8,128)} %refs_1_.1, s32[128,128]{1,0:T(8,128)} %bitcast.4, s32[4,128]{1,0:T(4,128)} %broadcast_in_dim.2.refs_3_, bf16[128,256]{1,0:T(8,128)(2,1)} %constant.33.clone.refs_4_, f32[2,8,128]{2,1,0:T(8,128)} %constant.34.clone.refs_5_, ...), custom_call_target="tpu_custom_call" | custom-call | tf_op jit(solution)/shard_map/pallas_call | solution.py:543
  86.3 1.6 %copy.12 = f32[8,4,1024]{2,1,0:T(4,128)} copy(f32[8,4,1024]{2,0,1:T(8,128)} %bitcast.3) | data formatting | bytes 262144 | tf_op jit(solution)/shard_map/reshape | solution.py:578
